TPU v7x, 256 devices: a 8x8x2 block of a 8x8x16 slice. The times are simulated.
256 devices in a mesh: grp: 2 (over z), trn: 64 (over y, x), tst: 2 (over core).
Axes of the slice: x: 8, y: 8, z: 2, core: 2. Of those that a mesh axis runs over, the one named last changes fastest.
The devices are a block of a 8x8x16 slice.
Arguments:
- test_points: bfloat16 [64, 8192], P(None, ('grp', 'tst')), parts along dimension 1, may hold values from -9 to 9
- train_points: bfloat16 [64, 524288], P(None, ('grp', 'trn')), parts along dimension 1, may hold values from -6 to 6
- weights: bfloat16 [524288], P(('grp', 'trn')), parts along dimension 0, may hold values from -6 to 6
- factor: bfloat16 [524288, 512], P(('grp', 'trn')), parts along dimension 0, may hold values from -1.14904852 to 1.14904852
Outputs:
- mean: float32 [8192], P(('grp', 'tst')), parts along dimension 0
- variance: float32 [8192], P(('grp', 'tst')), parts along dimension 0
There are 2 independent parts, one for each index of `grp`. A program takes and returns all parts, laid end to end along the dimension named above; each array names one. Nothing has to cross between parts.
All inputs are finite; a program needn't handle non-finite values.
Results may differ from a plain program's by a relative error of at most 0.0033.
Values sent between devices are 32-bit elements; how exact they have to be, the bound alone decides.
A program may use at most 64 MiB of HBM per device.

v0:
```python
import math
import jax
import jax.numpy as jnp
from jax import lax
from jax.sharding import Mesh
from jax.sharding import PartitionSpec as P

TRN = ("trn_0", "trn_1")
GRP_TRN = ("grp", "trn_0", "trn_1")


def scatter_axes(shard, axes, dim):
    if not axes:
        return shard
    nearer = lax.psum_scatter(shard, axes[0], scatter_dimension=dim, tiled=True)
    return scatter_axes(nearer, axes[1:], dim)


def turned_gather(arrays, axis, dims):
    turned = [jnp.moveaxis(a, dim, 0) for a, dim in zip(arrays, dims)]
    both = jnp.concatenate([t.reshape(len(t), -1) for t in turned], axis=1)
    result, at, outs = (lax.all_gather(both, axis, axis=0, tiled=True), 0, [])
    for t, dim in zip(turned, dims):
        piece = result[:, at : at + t[0].size].reshape(-1, *t.shape[1:])
        outs.append(jnp.moveaxis(piece, 0, dim))
        at += t[0].size
    return tuple(outs)


def on_device(test_points, train_points, weights, factor):
    rows = test_points.shape[1]
    local = train_points.shape[1]
    dim = test_points.shape[0]
    width = factor.shape[1]
    test_sq = jnp.sum(test_points.astype(jnp.float32) ** 2, axis=0)
    block = math.gcd(local, 1024)
    turns = local // block

    def step(index, carry):
        mean_acc, proj_acc = carry
        start = (index * block).astype(jnp.int32)
        points = lax.dynamic_slice_in_dim(train_points, start, block, 1)
        wblock = lax.dynamic_slice_in_dim(weights, start, block, 0)
        fblock = lax.dynamic_slice_in_dim(factor, start, block, 0)
        train_sq = jnp.sum(points.astype(jnp.float32) ** 2, axis=0)
        cross = lax.dot_general(
            test_points, points, (((0,), (0,)), ((), ())), preferred_element_type=jnp.float32
        )
        kernel = jnp.exp(
            -(test_sq[:, None] + train_sq[None, :] - 2.0 * cross) * (4.0 / dim)
        ).astype(jnp.bfloat16)
        mean_acc = mean_acc + jnp.dot(kernel, wblock, preferred_element_type=jnp.float32)
        proj_acc = proj_acc + jnp.dot(kernel, fblock, preferred_element_type=jnp.float32)
        return (mean_acc, proj_acc)

    init = (jnp.zeros((rows,), jnp.float32), jnp.zeros((rows, width), jnp.float32))
    mean_part, proj_part = lax.fori_loop(0, turns, step, init)
    mean_share, proj_share = (scatter_axes(mean_part, TRN, 0), scatter_axes(proj_part, TRN, 0))
    var_share = 1.0 - jnp.sum(proj_share * proj_share, axis=1)
    mean, variance = turned_gather((mean_share, var_share), TRN, (0, 0))
    return (mean, variance)


def solution(mesh):
    split = Mesh(
        mesh.devices.reshape(mesh.shape["grp"], 8, 8, mesh.shape["tst"]),
        ("grp", "trn_0", "trn_1", "tst"),
    )
    in_specs = (P(None, ("grp", "tst")), P(None, GRP_TRN), P(GRP_TRN), P(GRP_TRN, None))
    out_specs = (P(("grp", "tst")), P(("grp", "tst")))
    return jax.shard_map(
        on_device, mesh=split, in_specs=in_specs, out_specs=out_specs, check_vma=False
    )
```

profile of v0, /device:TPU:514, one launch (start us, length us, event | category | flops | bytes accessed | tf_op | source)
XLA Modules:
  0.0 241.4 jit_solution(6877016414136777848)
XLA Ops:
  7.3 1.0 multiply_reduce_fusion.1
  8.3 61.1 %while.16 = (s32[]{:T(128)}, f32[2048]{0:T(1024)S(1)}, f32[2048,512]{1,0:T(8,128)}, f32[2048]{0:T(1024)S(1)}, bf16[64,4096]{1,0:T(8,128)(2,1)}, /*index=5*/bf16[...) while((s32[]{:T(128)}, f32[2048]{0:T(1024)S(1)}, ...), condition=%wide.region_3.0_spmd.clone, body=%wide.region_1.0_spmd.clone.sunk | while | flops 2434993152 | bytes 39381208 | solution.py:57
  8.3 0.9 multiply_reduce_fusion.4
  9.3 5.0 %fusion.28 = bf16[2048,1024]{0,1:T(8,128)(2,1)} fusion(bf16[64,2048]{1,0:T(8,128)(2,1)} %get-tuple-element.267, f32[1024]{0:T(1024)S(1)} %multiply_reduce_fusion.4, f32[2048]{0:T(1024)S(1)} %get-tuple-element.265, bf16[64,4096]{1,0:T(8,128)(2,1)} %get-tuple-element.266, s32[]{:T(128)S(6)} %select_n.11), kind=kOutput, calls=%fused_computation.4.clone.1 | convolution fusion | flops 281018368 | bytes 4599812 | tf_op jit(solution)/shard_map/while/body/eval_jaxpr/dot_general | solution.py:46
  14.3 7.0 %select_add_fusion.5 = f32[2048,512]{1,0:T(8,128)} fusion(f32[2048,512]{1,0:T(8,128)} %get-tuple-element.252, bf16[2048,1024]{0,1:T(8,128)(2,1)} %fusion.28, pred[]{:T(512)S(6)} %compare.3, bf16[4096,512]{1,0:T(8,128)(2,1)} %get-tuple-element.269, s32[]{:T(128)S(6)} %select_n.11), kind=kOutput, calls=%fused_computation.5.clone.1 | convolution fusion | flops 2149580800 | bytes 13631493 | tf_op jit(solution)/shard_map/while/body/eval_jaxpr/dot_general | solution.py:53
  21.3 0.7 dynamic_slice.36
  21.9 0.7 fusion.29
  22.6 0.9 multiply_reduce_fusion.4
  23.6 5.0 %fusion.28 = bf16[2048,1024]{0,1:T(8,128)(2,1)} fusion(bf16[64,2048]{1,0:T(8,128)(2,1)} %get-tuple-element.267, f32[1024]{0:T(1024)S(1)} %multiply_reduce_fusion.4, f32[2048]{0:T(1024)S(1)} %get-tuple-element.265, bf16[64,4096]{1,0:T(8,128)(2,1)} %get-tuple-element.266, s32[]{:T(128)S(6)} %select_n.11), kind=kOutput, calls=%fused_computation.4.clone.1 | convolution fusion | flops 281018368 | bytes 4599812 | tf_op jit(solution)/shard_map/while/body/eval_jaxpr/dot_general | solution.py:46
  28.6 8.3 %select_add_fusion.5 = f32[2048,512]{1,0:T(8,128)} fusion(f32[2048,512]{1,0:T(8,128)} %get-tuple-element.252, bf16[2048,1024]{0,1:T(8,128)(2,1)} %fusion.28, pred[]{:T(512)S(6)} %compare.3, bf16[4096,512]{1,0:T(8,128)(2,1)} %get-tuple-element.269, s32[]{:T(128)S(6)} %select_n.11), kind=kOutput, calls=%fused_computation.5.clone.1 | convolution fusion | flops 2149580800 | bytes 13631493 | tf_op jit(solution)/shard_map/while/body/eval_jaxpr/dot_general | solution.py:53
  36.8 0.7 dynamic_slice.36
  37.5 0.7 fusion.29
  38.2 0.9 multiply_reduce_fusion.4
  39.1 5.0 %fusion.28 = bf16[2048,1024]{0,1:T(8,128)(2,1)} fusion(bf16[64,2048]{1,0:T(8,128)(2,1)} %get-tuple-element.267, f32[1024]{0:T(1024)S(1)} %multiply_reduce_fusion.4, f32[2048]{0:T(1024)S(1)} %get-tuple-element.265, bf16[64,4096]{1,0:T(8,128)(2,1)} %get-tuple-element.266, s32[]{:T(128)S(6)} %select_n.11), kind=kOutput, calls=%fused_computation.4.clone.1 | convolution fusion | flops 281018368 | bytes 4599812 | tf_op jit(solution)/shard_map/while/body/eval_jaxpr/dot_general | solution.py:46
  44.1 8.3 %select_add_fusion.5 = f32[2048,512]{1,0:T(8,128)} fusion(f32[2048,512]{1,0:T(8,128)} %get-tuple-element.252, bf16[2048,1024]{0,1:T(8,128)(2,1)} %fusion.28, pred[]{:T(512)S(6)} %compare.3, bf16[4096,512]{1,0:T(8,128)(2,1)} %get-tuple-element.269, s32[]{:T(128)S(6)} %select_n.11), kind=kOutput, calls=%fused_computation.5.clone.1 | convolution fusion | flops 2149580800 | bytes 13631493 | tf_op jit(solution)/shard_map/while/body/eval_jaxpr/dot_general | solution.py:53
  52.4 0.7 dynamic_slice.36
  53.1 0.7 fusion.29
  53.8 0.9 multiply_reduce_fusion.4
  54.7 5.0 %fusion.28 = bf16[2048,1024]{0,1:T(8,128)(2,1)} fusion(bf16[64,2048]{1,0:T(8,128)(2,1)} %get-tuple-element.267, f32[1024]{0:T(1024)S(1)} %multiply_reduce_fusion.4, f32[2048]{0:T(1024)S(1)} %get-tuple-element.265, bf16[64,4096]{1,0:T(8,128)(2,1)} %get-tuple-element.266, s32[]{:T(128)S(6)} %select_n.11), kind=kOutput, calls=%fused_computation.4.clone.1 | convolution fusion | flops 281018368 | bytes 4599812 | tf_op jit(solution)/shard_map/while/body/eval_jaxpr/dot_general | solution.py:46
  59.7 8.3 %select_add_fusion.5 = f32[2048,512]{1,0:T(8,128)} fusion(f32[2048,512]{1,0:T(8,128)} %get-tuple-element.252, bf16[2048,1024]{0,1:T(8,128)(2,1)} %fusion.28, pred[]{:T(512)S(6)} %compare.3, bf16[4096,512]{1,0:T(8,128)(2,1)} %get-tuple-element.269, s32[]{:T(128)S(6)} %select_n.11), kind=kOutput, calls=%fused_computation.5.clone.1 | convolution fusion | flops 2149580800 | bytes 13631493 | tf_op jit(solution)/shard_map/while/body/eval_jaxpr/dot_general | solution.py:53
  68.0 0.7 dynamic_slice.36
  68.7 0.7 fusion.29
  69.5 74.6 %reduce-scatter.3.cloned.1.call-done = f32[256,512]{1,0:T(8,128)} async-done(((f32[2048,512]{1,0:T(8,128)}), f32[256,512]{1,0:T(8,128)}) %reduce-scatter.3.cloned.1.call-update) | async-done | bytes 524304 | tf_op jit(solution)/shard_map/reduce_scatter | solution.py:15
  144.2 0.6 dynamic-slice
  145.4 0.6 dynamic-slice.2
  146.0 15.8 %all-reduce = f32[2048]{0:T(1024)S(1)} all-reduce(f32[2048]{0:T(1024)S(1)} %get-tuple-element.142), channel_id=2, replica_groups=mesh['grp'=2,'trn_0'=8,'trn_1'=8,'tst'=2] {'trn_0'}, use_global_device_ids=true, to_apply=%region_4.0.clone | all-reduce | flops 2048 | bytes 16384
  162.5 15.7 %all-reduce.1 = f32[256]{0:T(256)S(1)} all-reduce(f32[256]{0:T(256)S(1)} %dynamic-slice.1), channel_id=3, replica_groups=mesh['grp'=2,'trn_0'=8,'trn_1'=8,'tst'=2] {'trn_1'}, use_global_device_ids=true, to_apply=%region_5.0.clone | all-reduce | flops 256 | bytes 2048
  178.3 5.4 %reduce-scatter.5.cloned.1.call-done = f32[32,512]{1,0:T(8,128)} async-done(((f32[256,512]{1,0:T(8,128)}), f32[32,512]{1,0:T(8,128)}) %reduce-scatter.5.cloned.1.call-update) | async-done | bytes 65552 | tf_op jit(solution)/shard_map/reduce_scatter | solution.py:15
  183.7 1.0 multiply_reduce_fusion.2
  184.7 49.1 %all-gather = f32[64,32,2]{1,2,0:T(2,128)S(1)} all-gather(f32[1,32,2]{1,2,0:T(2,128)S(1)} %maximum_bitcast_fusion), channel_id=1, replica_groups=mesh['grp'=2,'trn_0'=8,'trn_1'=8,'tst'=2] {'trn_0','trn_1'}, dimensions={0}, use_global_device_ids=true | all-gather | bytes 16640 | tf_op jit(solution)/shard_map/all_gather | solution.py:22
  233.8 0.1 reshape.29
  233.9 0.6 fusion.8
  (31 shorter events, 0.5 us)
Async XLA Ops:
  7.2 136.9 %reduce-scatter.3.cloned.1.call-start = ((), (), s32[]{:S(2)}) async-start(), calls=%async_computation.2 | async-start | bytes 4718592 | tf_op jit(solution)/shard_map/reduce_scatter | solution.py:15
  14.3 7.7 %copy-start = (bf16[2048,1024]{0,1:T(8,128)(2,1)S(1)}, bf16[2048,1024]{0,1:T(8,128)(2,1)}, u32[]{:S(2)}) copy-start(bf16[2048,1024]{0,1:T(8,128)(2,1)} %fusion.28) | copy-start | bytes 12582916 | tf_op jit(solution)/shard_map/while
  28.6 9.0 %copy-start = (bf16[2048,1024]{0,1:T(8,128)(2,1)S(1)}, bf16[2048,1024]{0,1:T(8,128)(2,1)}, u32[]{:S(2)}) copy-start(bf16[2048,1024]{0,1:T(8,128)(2,1)} %fusion.28) | copy-start | bytes 12582916 | tf_op jit(solution)/shard_map/while
  44.1 9.0 %copy-start = (bf16[2048,1024]{0,1:T(8,128)(2,1)S(1)}, bf16[2048,1024]{0,1:T(8,128)(2,1)}, u32[]{:S(2)}) copy-start(bf16[2048,1024]{0,1:T(8,128)(2,1)} %fusion.28) | copy-start | bytes 12582916 | tf_op jit(solution)/shard_map/while
  59.7 9.0 %copy-start = (bf16[2048,1024]{0,1:T(8,128)(2,1)S(1)}, bf16[2048,1024]{0,1:T(8,128)(2,1)}, u32[]{:S(2)}) copy-start(bf16[2048,1024]{0,1:T(8,128)(2,1)} %fusion.28) | copy-start | bytes 12582916 | tf_op jit(solution)/shard_map/while
  69.3 74.8 %copy-start.2 = (u32[256]{0:T(256)S(1)}, u32[256]{0:T(256)}, u32[]{:S(2)}) copy-start(u32[256]{0:T(256)} %constant.56) | copy-start | bytes 3076
  69.4 76.1 %copy-start.1 = (u32[256]{0:T(256)S(1)}, u32[256]{0:T(256)}, u32[]{:S(2)}) copy-start(u32[256]{0:T(256)} %constant.60) | copy-start | bytes 3076
  69.4 114.3 %reduce-scatter.5.cloned.1.call-start = ((), (), s32[]{:S(2)}) async-start(), calls=%async_computation.3 | async-start | bytes 589824 | tf_op jit(solution)/shard_map/reduce_scatter | solution.py:15
Sparse Core Ops, SparseCore 0:
  69.5 74.5 reduce-scatter.2
  146.7 37.0 reduce-scatter.4
where the time goes:
time: 242 us; the launch traced here: 241 us
  blocking collectives  80.6 us (33%)
  waiting for transfers between devices  80.1 us (33%)
  matrix products  54.4 us (22%)
  between operations  15.4 us (6%)
  other arithmetic  5.82 us (2%)
  local copies, waits for them, and re-layouts  4.83 us (2%)
    reduce_scatter x2, waiting for transfers between devices, scatter_axes(): nearer = lax.psum_scatter(shard, axes[0], scatter_dimension=dim, tiled=True)  80 us
    all_gather x1, blocking collectives, turned_gather(): result, at, outs = (lax.all_gather(both, axis, axis=0, tiled=True), 0, [])  49.1 us
    dot_general x4, matrix products, step(): jnp.dot(kernel, fblock, preferred_element_type=jnp.float32)  31.8 us
    unnamed x2, blocking collectives  31.5 us
    dot_general x4, matrix products, step(): lax.dot_general(test_points, points, (((0,), (0,)), ((), ())), preferred_...  20 us
  transfers between devices with their start and end apart: 2, of which 2 were waited for; matrix products, arithmetic and copies ran while one was open for 1% of the time, Pallas kernels for 0%

commit v1 on v0

--- a/solution.py
+++ b/solution.py
@@ -19,7 +19,13 @@
 def turned_gather(arrays, axis, dims):
     turned = [jnp.moveaxis(a, dim, 0) for a, dim in zip(arrays, dims)]
     both = jnp.concatenate([t.reshape(len(t), -1) for t in turned], axis=1)
-    result, at, outs = (lax.all_gather(both, axis, axis=0, tiled=True), 0, [])
+    result, at, outs = (
+        jnp.concatenate(
+            lax.all_to_all(jnp.stack([both] * lax.axis_size(axis)), axis, 0, 0), axis=0
+        ),
+        0,
+        [],
+    )
     for t, dim in zip(turned, dims):
         piece = result[:, at : at + t[0].size].reshape(-1, *t.shape[1:])
         outs.append(jnp.moveaxis(piece, 0, dim))

time: 242 us -> 216 us (0.89)
  blocking collectives: 80.6 us -> 54.2 us
    all_gather x1 -> x0, blocking collectives: 49.1 us -> none  [turned_gather(): result, at, outs = (lax.all_gather(both, axis, axis=0, tiled=True), 0, [])]
    all_to_all x0 -> x1, blocking collectives: none -> 22.8 us  [turned_gather(): lax.all_to_all(jnp.stack([both] * lax.axis_size(axis)), axis, 0, 0)]
where the time goes in v1:
time: 216 us; the launch traced here: 215 us
  waiting for transfers between devices  80.1 us (37%)
  matrix products  54.4 us (25%)
  blocking collectives  54.2 us (25%)
  between operations  15.4 us (7%)
  other arithmetic  5.82 us (3%)
  local copies, waits for them, and re-layouts  4.85 us (2%)
    reduce_scatter x2, waiting for transfers between devices, scatter_axes(): nearer = lax.psum_scatter(shard, axes[0], scatter_dimension=dim, tiled=True)  80 us
    dot_general x4, matrix products, step(): jnp.dot(kernel, fblock, preferred_element_type=jnp.float32)  31.8 us
    unnamed x2, blocking collectives  31.5 us
    all_to_all x1, blocking collectives, turned_gather(): lax.all_to_all(jnp.stack([both] * lax.axis_size(axis)), axis, 0, 0)  22.8 us
    dot_general x4, matrix products, step(): lax.dot_general(test_points, points, (((0,), (0,)), ((), ())), preferred_...  20 us
  transfers between devices with their start and end apart: 2, of which 2 were waited for; matrix products, arithmetic and copies ran while one was open for 1% of the time, Pallas kernels for 0%

profile of v1, /device:TPU:514, one launch (start us, length us, event | category | flops | bytes accessed | tf_op | source)
XLA Modules:
  0.0 215.0 jit_solution(6810002341641825721)
XLA Ops:
  7.3 1.0 multiply_reduce_fusion.1
  8.3 61.1 %while.16 = (s32[]{:T(128)}, f32[2048]{0:T(1024)S(1)}, f32[2048,512]{1,0:T(8,128)}, f32[2048]{0:T(1024)S(1)}, bf16[64,4096]{1,0:T(8,128)(2,1)}, /*index=5*/bf16[...) while((s32[]{:T(128)}, f32[2048]{0:T(1024)S(1)}, ...), condition=%wide.region_3.0_spmd.clone, body=%wide.region_1.0_spmd.clone.sunk | while | flops 2434993152 | bytes 39381208 | solution.py:63
  8.3 0.9 multiply_reduce_fusion.4
  9.3 5.0 %fusion.28 = bf16[2048,1024]{0,1:T(8,128)(2,1)} fusion(bf16[64,2048]{1,0:T(8,128)(2,1)} %get-tuple-element.267, f32[1024]{0:T(1024)S(1)} %multiply_reduce_fusion.4, f32[2048]{0:T(1024)S(1)} %get-tuple-element.265, bf16[64,4096]{1,0:T(8,128)(2,1)} %get-tuple-element.266, s32[]{:T(128)S(6)} %select_n.11), kind=kOutput, calls=%fused_computation.4.clone.1 | convolution fusion | flops 281018368 | bytes 4599812 | tf_op jit(solution)/shard_map/while/body/eval_jaxpr/dot_general | solution.py:52
  14.3 7.0 %select_add_fusion.5 = f32[2048,512]{1,0:T(8,128)} fusion(f32[2048,512]{1,0:T(8,128)} %get-tuple-element.252, bf16[2048,1024]{0,1:T(8,128)(2,1)} %fusion.28, pred[]{:T(512)S(6)} %compare.3, bf16[4096,512]{1,0:T(8,128)(2,1)} %get-tuple-element.269, s32[]{:T(128)S(6)} %select_n.11), kind=kOutput, calls=%fused_computation.5.clone.1 | convolution fusion | flops 2149580800 | bytes 13631493 | tf_op jit(solution)/shard_map/while/body/eval_jaxpr/dot_general | solution.py:59
  21.3 0.7 dynamic_slice.36
  21.9 0.7 fusion.29
  22.6 0.9 multiply_reduce_fusion.4
  23.6 5.0 %fusion.28 = bf16[2048,1024]{0,1:T(8,128)(2,1)} fusion(bf16[64,2048]{1,0:T(8,128)(2,1)} %get-tuple-element.267, f32[1024]{0:T(1024)S(1)} %multiply_reduce_fusion.4, f32[2048]{0:T(1024)S(1)} %get-tuple-element.265, bf16[64,4096]{1,0:T(8,128)(2,1)} %get-tuple-element.266, s32[]{:T(128)S(6)} %select_n.11), kind=kOutput, calls=%fused_computation.4.clone.1 | convolution fusion | flops 281018368 | bytes 4599812 | tf_op jit(solution)/shard_map/while/body/eval_jaxpr/dot_general | solution.py:52
  28.6 8.3 %select_add_fusion.5 = f32[2048,512]{1,0:T(8,128)} fusion(f32[2048,512]{1,0:T(8,128)} %get-tuple-element.252, bf16[2048,1024]{0,1:T(8,128)(2,1)} %fusion.28, pred[]{:T(512)S(6)} %compare.3, bf16[4096,512]{1,0:T(8,128)(2,1)} %get-tuple-element.269, s32[]{:T(128)S(6)} %select_n.11), kind=kOutput, calls=%fused_computation.5.clone.1 | convolution fusion | flops 2149580800 | bytes 13631493 | tf_op jit(solution)/shard_map/while/body/eval_jaxpr/dot_general | solution.py:59
  36.8 0.7 dynamic_slice.36
  37.5 0.7 fusion.29
  38.2 0.9 multiply_reduce_fusion.4
  39.1 5.0 %fusion.28 = bf16[2048,1024]{0,1:T(8,128)(2,1)} fusion(bf16[64,2048]{1,0:T(8,128)(2,1)} %get-tuple-element.267, f32[1024]{0:T(1024)S(1)} %multiply_reduce_fusion.4, f32[2048]{0:T(1024)S(1)} %get-tuple-element.265, bf16[64,4096]{1,0:T(8,128)(2,1)} %get-tuple-element.266, s32[]{:T(128)S(6)} %select_n.11), kind=kOutput, calls=%fused_computation.4.clone.1 | convolution fusion | flops 281018368 | bytes 4599812 | tf_op jit(solution)/shard_map/while/body/eval_jaxpr/dot_general | solution.py:52
  44.1 8.3 %select_add_fusion.5 = f32[2048,512]{1,0:T(8,128)} fusion(f32[2048,512]{1,0:T(8,128)} %get-tuple-element.252, bf16[2048,1024]{0,1:T(8,128)(2,1)} %fusion.28, pred[]{:T(512)S(6)} %compare.3, bf16[4096,512]{1,0:T(8,128)(2,1)} %get-tuple-element.269, s32[]{:T(128)S(6)} %select_n.11), kind=kOutput, calls=%fused_computation.5.clone.1 | convolution fusion | flops 2149580800 | bytes 13631493 | tf_op jit(solution)/shard_map/while/body/eval_jaxpr/dot_general | solution.py:59
  52.4 0.7 dynamic_slice.36
  53.1 0.7 fusion.29
  53.8 0.9 multiply_reduce_fusion.4
  54.7 5.0 %fusion.28 = bf16[2048,1024]{0,1:T(8,128)(2,1)} fusion(bf16[64,2048]{1,0:T(8,128)(2,1)} %get-tuple-element.267, f32[1024]{0:T(1024)S(1)} %multiply_reduce_fusion.4, f32[2048]{0:T(1024)S(1)} %get-tuple-element.265, bf16[64,4096]{1,0:T(8,128)(2,1)} %get-tuple-element.266, s32[]{:T(128)S(6)} %select_n.11), kind=kOutput, calls=%fused_computation.4.clone.1 | convolution fusion | flops 281018368 | bytes 4599812 | tf_op jit(solution)/shard_map/while/body/eval_jaxpr/dot_general | solution.py:52
  59.7 8.3 %select_add_fusion.5 = f32[2048,512]{1,0:T(8,128)} fusion(f32[2048,512]{1,0:T(8,128)} %get-tuple-element.252, bf16[2048,1024]{0,1:T(8,128)(2,1)} %fusion.28, pred[]{:T(512)S(6)} %compare.3, bf16[4096,512]{1,0:T(8,128)(2,1)} %get-tuple-element.269, s32[]{:T(128)S(6)} %select_n.11), kind=kOutput, calls=%fused_computation.5.clone.1 | convolution fusion | flops 2149580800 | bytes 13631493 | tf_op jit(solution)/shard_map/while/body/eval_jaxpr/dot_general | solution.py:59
  68.0 0.7 dynamic_slice.36
  68.7 0.7 fusion.29
  69.5 74.6 %reduce-scatter.3.cloned.1.call-done = f32[256,512]{1,0:T(8,128)} async-done(((f32[2048,512]{1,0:T(8,128)}), f32[256,512]{1,0:T(8,128)}) %reduce-scatter.3.cloned.1.call-update) | async-done | bytes 524304 | tf_op jit(solution)/shard_map/reduce_scatter | solution.py:15
  144.2 0.6 dynamic-slice
  145.4 0.6 dynamic-slice.2
  146.0 15.8 %all-reduce = f32[2048]{0:T(1024)S(1)} all-reduce(f32[2048]{0:T(1024)S(1)} %get-tuple-element.142), channel_id=2, replica_groups=mesh['grp'=2,'trn_0'=8,'trn_1'=8,'tst'=2] {'trn_0'}, use_global_device_ids=true, to_apply=%region_4.0.clone | all-reduce | flops 2048 | bytes 16384
  162.5 15.7 %all-reduce.1 = f32[256]{0:T(256)S(1)} all-reduce(f32[256]{0:T(256)S(1)} %dynamic-slice.1), channel_id=3, replica_groups=mesh['grp'=2,'trn_0'=8,'trn_1'=8,'tst'=2] {'trn_1'}, use_global_device_ids=true, to_apply=%region_5.0.clone | all-reduce | flops 256 | bytes 2048
  178.3 5.4 %reduce-scatter.5.cloned.1.call-done = f32[32,512]{1,0:T(8,128)} async-done(((f32[256,512]{1,0:T(8,128)}), f32[32,512]{1,0:T(8,128)}) %reduce-scatter.5.cloned.1.call-update) | async-done | bytes 65552 | tf_op jit(solution)/shard_map/reduce_scatter | solution.py:15
  183.7 1.0 multiply_reduce_fusion.2
  184.7 22.8 %all_to_all.5 = f32[64,32,2]{1,2,0:T(2,128)S(1)} all-to-all(f32[64,32,2]{1,2,0:T(2,128)S(1)} %stack.2), channel_id=1, replica_groups=mesh['grp'=2,'trn_0'=8,'trn_1'=8,'tst'=2] {'trn_0','trn_1'}, dimensions={0} | all-to-all | bytes 32768 | tf_op jit(solution)/shard_map/all_to_all | solution.py:24
  207.5 0.1 reshape.31
  207.6 0.6 fusion.8
  (32 shorter events, 0.5 us)
Async XLA Ops:
  7.2 136.9 %reduce-scatter.3.cloned.1.call-start = ((), (), s32[]{:S(2)}) async-start(), calls=%async_computation.3 | async-start | bytes 4718592 | tf_op jit(solution)/shard_map/reduce_scatter | solution.py:15
  14.3 7.7 %copy-start = (bf16[2048,1024]{0,1:T(8,128)(2,1)S(1)}, bf16[2048,1024]{0,1:T(8,128)(2,1)}, u32[]{:S(2)}) copy-start(bf16[2048,1024]{0,1:T(8,128)(2,1)} %fusion.28) | copy-start | bytes 12582916 | tf_op jit(solution)/shard_map/while
  28.6 9.0 %copy-start = (bf16[2048,1024]{0,1:T(8,128)(2,1)S(1)}, bf16[2048,1024]{0,1:T(8,128)(2,1)}, u32[]{:S(2)}) copy-start(bf16[2048,1024]{0,1:T(8,128)(2,1)} %fusion.28) | copy-start | bytes 12582916 | tf_op jit(solution)/shard_map/while
  44.1 9.0 %copy-start = (bf16[2048,1024]{0,1:T(8,128)(2,1)S(1)}, bf16[2048,1024]{0,1:T(8,128)(2,1)}, u32[]{:S(2)}) copy-start(bf16[2048,1024]{0,1:T(8,128)(2,1)} %fusion.28) | copy-start | bytes 12582916 | tf_op jit(solution)/shard_map/while
  59.7 9.0 %copy-start = (bf16[2048,1024]{0,1:T(8,128)(2,1)S(1)}, bf16[2048,1024]{0,1:T(8,128)(2,1)}, u32[]{:S(2)}) copy-start(bf16[2048,1024]{0,1:T(8,128)(2,1)} %fusion.28) | copy-start | bytes 12582916 | tf_op jit(solution)/shard_map/while
  69.3 74.8 %copy-start.2 = (u32[256]{0:T(256)S(1)}, u32[256]{0:T(256)}, u32[]{:S(2)}) copy-start(u32[256]{0:T(256)} %constant.56) | copy-start | bytes 3076
  69.4 76.1 %copy-start.1 = (u32[256]{0:T(256)S(1)}, u32[256]{0:T(256)}, u32[]{:S(2)}) copy-start(u32[256]{0:T(256)} %constant.60) | copy-start | bytes 3076
  69.4 114.3 %reduce-scatter.5.cloned.1.call-start = ((), (), s32[]{:S(2)}) async-start(), calls=%async_computation.4 | async-start | bytes 589824 | tf_op jit(solution)/shard_map/reduce_scatter | solution.py:15
Sparse Core Ops, SparseCore 0:
  69.5 74.5 reduce-scatter.2
  146.7 37.0 reduce-scatter.4
